TPU v7x, 256 devices: a whole 4x4x8 slice. The times are simulated.
256 devices in a mesh: ctx: 64 (over z, y, core), head: 4 (over x).
Axes of the slice: x: 4, y: 4, z: 8, core: 2. Of those that a mesh axis runs over, the one named last changes fastest.
Arguments:
- query_latent: bfloat16 [128, 128, 576], P(None, 'head'), may hold values from -7 to 7
- key_latent: bfloat16 [131072, 576], P('ctx'), may hold values from -6 to 6
- index_query: bfloat16 [128, 64, 128], P(None, 'head'), may hold values from -0.5 to 0.5
- index_weight: bfloat16 [128, 64], P(None, 'head'), may hold values from -110 to 110
- index_key: bfloat16 [131072, 128], P('ctx'), may hold values from -6 to 6
- positions: int32 [128], replicated, may hold values from 32768 to 131071
Outputs:
- target: float32 [128, 131072], P('head', 'ctx')
- divergence: float32 [128], P('head')
Inputs may be any that keep to these rules, and one draw needn't show every extreme that they name: Row q may attend to keys 0 through positions[q].
All inputs are finite; a program needn't handle non-finite values.
Results may differ from a plain program's by a relative error of at most 0.0003.
Values may be sent and summed in bfloat16 or wider, within the bound.
A program may use at most 128 MiB of HBM per device.

v0:
```python
import math

import jax
import jax.numpy as jnp
from jax import lax
from jax.sharding import Mesh
from jax.sharding import PartitionSpec as P

H = 128
CTX = ("ctx_0", "ctx_1", "ctx_2")


def side_by_side(arrays, axis, split_dim, concat_dim, along):
    widths = [math.prod(a.shape[along:]) for a in arrays]
    both = jnp.concatenate(
        [a.reshape(*a.shape[:along], w) for a, w in zip(arrays, widths)], axis=along
    )
    out = lax.all_to_all(both, axis, split_axis=split_dim, concat_axis=concat_dim, tiled=True)
    pieces = jnp.split(out, [sum(widths[:k]) for k in range(1, len(widths))], axis=along)
    return tuple((b.reshape(*out.shape[:along], *a.shape[along:]) for a, b in zip(arrays, pieces)))


def gathered_once(shard, axis):
    leaves = jax.tree.leaves(shard)
    turns = sorted(range(len(leaves)), key=lambda k: -leaves[k].size)
    width = (1, *leaves[turns[0]].shape)[-1]
    lines = [
        jnp.pad(leaves[k].reshape(-1), (0, -leaves[k].size % width)).reshape(-1, width)
        for k in turns
    ]
    both, at, found = (lax.all_gather(jnp.concatenate(lines), axis), 0, {})
    for k, line in zip(turns, lines):
        piece = both[:, at : at + len(line)].reshape(len(both), -1)
        found[k] = piece[:, : leaves[k].size].reshape(-1, *leaves[k].shape)
        at += len(line)
    numbers = iter(range(len(leaves)))
    return jax.tree.map(lambda _: found[next(numbers)], shard)


def merged_by_axis(shard, axes, combine):
    for axis in axes:
        pieces = gathered_once(shard, axis)
        shard = jax.tree.map(lambda part: part[0], pieces)
        for k in range(1, lax.axis_size(axis)):
            shard = combine(shard, jax.tree.map(lambda part: part[k], pieces))
    return shard


def cut_along(shard, dim, count):
    before, after = (shard.shape[:dim], shard.shape[dim + 1 :])
    return jnp.moveaxis(shard.reshape(*before, count, -1, *after), dim, 0)


def sum_at_owner(shard, axis, dim):
    count = lax.axis_size(axis)
    pieces = lax.all_to_all(cut_along(shard, dim, count), axis, 0, 0, tiled=True)
    return jnp.sum(pieces, axis=0)


def from_everyone(shard, axis):
    copies = jnp.broadcast_to(shard, (lax.axis_size(axis), *shard.shape))
    return lax.all_to_all(copies, axis, split_axis=0, concat_axis=0, tiled=True)


def collected_together(shard, axis):
    leaves = jax.tree.leaves(shard)
    turns = sorted(range(len(leaves)), key=lambda k: -leaves[k].size)
    width = (1, *leaves[turns[0]].shape)[-1]
    lines = [
        jnp.pad(leaves[k].reshape(-1), (0, -leaves[k].size % width)).reshape(-1, width)
        for k in turns
    ]
    both, at, found = (from_everyone(jnp.concatenate(lines), axis), 0, {})
    for k, line in zip(turns, lines):
        piece = both[:, at : at + len(line)].reshape(len(both), -1)
        found[k] = piece[:, : leaves[k].size].reshape(-1, *leaves[k].shape)
        at += len(line)
    numbers = iter(range(len(leaves)))
    return jax.tree.map(lambda _: found[next(numbers)], shard)


def gathered_by_type(shard, axis):
    leaves, found = (jax.tree.leaves(shard), {})
    for leading, a in enumerate(leaves):
        if leading not in found:
            alike = [k for k, b in enumerate(leaves) if b.dtype == a.dtype]
            got = (
                collected_together([leaves[k] for k in alike], axis)
                if len(alike) > 1
                else [from_everyone(a, axis)]
            )
            for k, b in zip(alike, got):
                found[k] = b
    numbers = iter(range(len(leaves)))
    return jax.tree.map(lambda _: found[next(numbers)], shard)


def joined_by_halves(pieces, combine):
    while len(jax.tree.leaves(pieces)[0]) > 1:
        pieces = jax.vmap(combine)(
            *(jax.tree.map(lambda part: part[side::2], pieces) for side in (0, 1))
        )
    return jax.tree.map(lambda part: part[0], pieces)


def merged(shard, axis, combine):
    pieces = gathered_by_type(shard, axis)
    return joined_by_halves(pieces, combine)


def merge_pair(first, second):
    top_a, total_a = first
    top_b, total_b = second
    highest = jnp.maximum(top_a, top_b)
    return (highest, total_a * jnp.exp(top_a - highest) + total_b * jnp.exp(top_b - highest))


def merge_four(first, second):
    highest, total = merge_pair((first[0], first[1]), (second[0], second[1]))
    return (highest, total, first[2] + second[2], first[3] + second[3])


def local(query_latent, key_latent, index_query, index_weight, index_key, positions):
    keys_local = key_latent.shape[0]
    key_pos = lax.axis_index(CTX) * keys_local + jnp.arange(keys_local, dtype=jnp.int32)
    row_count = positions.shape[0] // lax.axis_size("head")
    own_rows = lax.dynamic_slice_in_dim(positions, lax.axis_index("head") * row_count, row_count)
    index_query, index_weight = side_by_side((index_query, index_weight), "head", 0, 1, 2)
    allowed = key_pos[None, :] <= positions[:, None]
    scores = jnp.einsum("qhd,kd->hqk", query_latent, key_latent, preferred_element_type=jnp.float32)
    local_top = jnp.max(jnp.where(allowed[None], scores, -1e30), axis=2)
    local_total = jnp.sum(
        jnp.where(allowed[None], jnp.exp(scores - local_top[:, :, None]), 0.0), axis=2
    )
    highest, total = merged_by_axis((local_top, local_total), CTX, merge_pair)
    weights = (
        jnp.where(allowed[None], jnp.exp(scores - highest[:, :, None]), 0.0) / total[:, :, None]
    )
    head_part = jnp.sum(weights, axis=0)
    raw_index = jnp.einsum(
        "qjd,kd->qjk", index_query, index_key, preferred_element_type=jnp.float32
    )
    logit_part = jnp.sum(
        index_weight.astype(jnp.float32)[:, :, None] * jnp.maximum(raw_index, 0.0), axis=1
    )
    summed = sum_at_owner(head_part, "head", 0)
    target = summed / H
    row_allowed = key_pos[None, :] <= own_rows[:, None]
    index_top = jnp.max(jnp.where(row_allowed, logit_part, -1e30), axis=1)
    positive = target > 0
    entropy_terms = jnp.where(positive, target * jnp.log(jnp.where(positive, target, 1.0)), 0.0)
    cross = jnp.sum(jnp.where(row_allowed, entropy_terms - target * logit_part, 0.0), axis=1)
    mass = jnp.sum(target, axis=1)
    index_total = jnp.sum(
        jnp.where(row_allowed, jnp.exp(logit_part - index_top[:, None]), 0.0), axis=1
    )
    peak, denom, cross, mass = merged((index_top, index_total, cross, mass), CTX, merge_four)
    divergence = cross + (peak + jnp.log(denom)) * mass
    return (target, divergence)


def solution(mesh):
    finer = Mesh(
        mesh.devices.reshape(8, 4, 2, mesh.shape["head"]), ("ctx_0", "ctx_1", "ctx_2", "head")
    )
    return jax.shard_map(
        local,
        mesh=finer,
        in_specs=(
            P(None, "head", None),
            P(CTX, None),
            P(None, "head", None),
            P(None, "head"),
            P(CTX, None),
            P(),
        ),
        out_specs=(P("head", CTX), P("head")),
        check_vma=False,
    )
```

profile of v0, /device:TPU:1, one launch (start us, length us, event | category | flops | bytes accessed | tf_op | source)
XLA Modules:
  0.0 139.0 jit_solution(8303171662838771580)
XLA Ops:
  0.6 0.0 copy-start
  0.6 1.3 copy.18
  1.9 2.2 %pad_maximum_fusion = bf16[128,16,129]{2,1,0:T(8,128)(2,1)} fusion(bf16[128,16,1]{2,1,0:T(8,128)(2,1)S(1)} %copy.18, bf16[128,16,128]{2,1,0:T(8,128)(2,1)} %param.8), kind=kLoop, calls=%fused_computation.14 | loop fusion | flops 1056768 | bytes 1056768 | tf_op jit(solution)/shard_map/concatenate | solution.py:15
  4.2 4.8 %all-to-all-start.1 = ((bf16[128,16,129]{2,1,0:T(8,128)(2,1)}), bf16[128,16,129]{2,1,0:T(8,128)(2,1)}, u32[]{:S(2)}, u32[]{:S(2)}) async-start(bf16[128,16,129]{2,1,0:T(8,128)(2,1)} %pad_maximum_fusion), calls=%async_computation.1 | async-start | bytes 2097152 | tf_op jit(solution)/shard_map/all_to_all | solution.py:18
  9.0 1.0 broadcast_compare_fusion
  10.0 19.6 %fusion = (f32[32,128]{1,0:T(8,128)S(1)}, f32[2048,128,32]{1,0,2:T(8,128)}) fusion(pred[128,2048]{0,1:T(8,128)(4,1)S(1)} %broadcast_compare_fusion, bf16[128,32,576]{0,2,1:T(8,128)(2,1)} %param.6, bf16[2048,576]{0,1:T(8,128)(2,1)S(1)} %copy-done), kind=kOutput, calls=%fused_computation.3 | convolution fusion | flops 9680449536 | bytes 40910848 | tf_op jit(solution)/shard_map/qhd,kd->hqk/dot_general | solution.py:130
  29.7 14.3 %fusion.3 = f32[32,128]{1,0:T(8,128)S(1)} fusion(f32[2048,128,32]{1,0,2:T(8,128)} %get-tuple-element.27, f32[32,128]{1,0:T(8,128)S(1)} %get-tuple-element.26, pred[128,2048]{0,1:T(8,128)(4,1)S(1)} %broadcast_compare_fusion), kind=kLoop, calls=%fused_computation.6 | loop fusion | flops 25161728 | bytes 33849344 | tf_op jit(solution)/shard_map/reduce_sum | solution.py:132
  44.0 22.9 %all-gather = f32[512,128]{1,0:T(8,128)S(1)} all-gather(f32[64,128]{1,0:T(8,128)S(1)} %pad_maximum_fusion.1), channel_id=2, replica_groups=mesh['ctx_0'=8,'ctx_1'=4,'ctx_2'=2,'head'=4] {'ctx_0'}, dimensions={0}, use_global_device_ids=true | all-gather | bytes 294912 | tf_op jit(solution)/shard_map/all_gather | solution.py:31
  66.9 9.9 %all-gather.1 = f32[256,128]{1,0:T(8,128)S(1)} all-gather(f32[64,128]{1,0:T(8,128)S(1)} %pad_maximum_fusion.2), channel_id=3, replica_groups=mesh['ctx_0'=8,'ctx_1'=4,'ctx_2'=2,'head'=4] {'ctx_1'}, dimensions={0}, use_global_device_ids=true | all-gather | bytes 163840 | tf_op jit(solution)/shard_map/all_gather | solution.py:31
  76.9 10.9 %all-gather.2 = f32[128,128]{1,0:T(8,128)S(1)} all-gather(f32[64,128]{1,0:T(8,128)S(1)} %pad_maximum_fusion.3), channel_id=4, replica_groups=mesh['ctx_0'=8,'ctx_1'=4,'ctx_2'=2,'head'=4] {'ctx_2'}, dimensions={0}, use_global_device_ids=true | all-gather | bytes 98304 | tf_op jit(solution)/shard_map/all_gather | solution.py:31
  87.8 0.0 copy-done.1
  87.8 0.0 copy-start.2
  87.8 7.0 %fusion.7 = f32[128,2048]{0,1:T(8,128)S(1)} fusion(f32[2048,128,32]{1,0,2:T(8,128)S(1)} %copy-done.1, f32[32,128]{1,0:T(8,128)S(1)} %get-tuple-element.16, f32[32,128]{1,0:T(8,128)S(1)} %get-tuple-element.17, pred[128,2048]{0,1:T(8,128)(4,1)S(1)} %broadcast_compare_fusion), kind=kLoop, calls=%fused_computation.10 | loop fusion | flops 33292288 | bytes 34897920 | tf_op jit(solution)/shard_map/reduce_sum | solution.py:139
  94.9 1.3 copy.17
  96.2 0.0 all-to-all-done.1
  96.2 4.4 %all-to-all-start = ((f32[4,32,2048]{2,1,0:T(8,128)}), f32[4,32,2048]{2,1,0:T(8,128)S(1)}, u32[]{:S(2)}, u32[]{:S(2)}) async-start(f32[4,32,2048]{2,1,0:T(8,128)} %bitcast.308), calls=%async_computation | async-start | bytes 2097152 | tf_op jit(solution)/shard_map/all_to_all | solution.py:56
  100.6 0.0 copy-done.2
  100.6 0.1 dynamic_slice.3
  100.7 1.4 copy.19
  102.0 0.3 convert_reduce_fusion
  102.4 4.4 %multiply_reduce_fusion = f32[32,2048]{1,0:T(8,128)} fusion(f32[32,64]{1,0:T(8,128)S(1)} %convert_reduce_fusion, bf16[32,64,129]{2,1,0:T(8,128)(2,1)S(1)} %bitcast.310, bf16[2048,128]{1,0:T(8,128)(2,1)} %param.10), kind=kOutput, calls=%fused_computation.11 | convolution fusion | flops 1086259200 | bytes 1327104 | tf_op jit(solution)/shard_map/qjd,kd->qjk/dot_general | solution.py:140
  106.8 1.2 fusion.15
  108.0 7.2 %all-to-all-done = f32[4,32,2048]{2,1,0:T(8,128)S(1)} async-done(((f32[4,32,2048]{2,1,0:T(8,128)}), f32[4,32,2048]{2,1,0:T(8,128)S(1)}, u32[]{:S(2)}, u32[]{:S(2)}) %all-to-all-start) | async-done | bytes 1048608 | tf_op jit(solution)/shard_map/all_to_all | solution.py:56
  115.2 0.8 reduce_sum.65
  115.9 2.0 %fusion.16 = (f32[32]{0:T(128)S(1)}, f32[32]{0:T(128)S(1)}, f32[32]{0:T(128)S(1)}, f32[32,2048]{1,0:T(8,128)}) fusion(f32[32,2048]{1,0:T(8,128)} %multiply_reduce_fusion, f32[32]{0:T(128)S(1)} %fusion.15, s32[2048]{0:T(1024)S(1)} %iota_add_fusion, s32[32]{0:T(128)S(1)} %dynamic_slice.3, f32[32,2048]{1,0:T(8,128)} %reduce_sum.65), kind=kLoop, calls=%fused_computation.28 | loop fusion | flops 917408 | bytes 795264 | tf_op jit(solution)/shard_map/reduce_sum | solution.py:154
  118.0 0.1 reshape.137
  118.1 18.0 %all_to_all.28 = f32[64,1,128]{2,1,0:T(1,128)S(1)} all-to-all(f32[64,1,128]{2,1,0:T(1,128)S(1)} %reshape.137), channel_id=1, replica_groups=mesh['ctx_0'=8,'ctx_1'=4,'ctx_2'=2,'head'=4] {'ctx_0','ctx_1','ctx_2'}, dimensions={0} | all-to-all | bytes 65536 | tf_op jit(solution)/shard_map/all_to_all | solution.py:62
  136.1 0.5 broadcast.27
  136.6 0.7 reduce.2
  137.3 0.1 reshape.138
  137.5 0.1 fusion.67
  138.5 0.5 add_bitcast_fusion
  (66 shorter events, 1.0 us)
Async XLA Ops:
  0.6 9.4 %copy-start = (bf16[2048,576]{0,1:T(8,128)(2,1)S(1)}, bf16[2048,576]{0,1:T(8,128)(2,1)}, u32[]{:S(2)}) copy-start(bf16[2048,576]{0,1:T(8,128)(2,1)} %param.7) | copy-start | bytes 7077892
  4.2 92.0 %all-to-all-start.1 = ((bf16[128,16,129]{2,1,0:T(8,128)(2,1)}), bf16[128,16,129]{2,1,0:T(8,128)(2,1)}, u32[]{:S(2)}, u32[]{:S(2)}) async-start(bf16[128,16,129]{2,1,0:T(8,128)(2,1)} %pad_maximum_fusion), calls=%async_computation.1 | async-start | bytes 2097152 | tf_op jit(solution)/shard_map/all_to_all | solution.py:18
  29.7 58.1 %copy-start.1 = (f32[2048,128,32]{1,0,2:T(8,128)S(1)}, f32[2048,128,32]{1,0,2:T(8,128)}, u32[]{:S(2)}) copy-start(f32[2048,128,32]{1,0,2:T(8,128)} %get-tuple-element.27) | copy-start | bytes 100663296
  87.8 12.8 %copy-start.2 = (s32[128]{0:T(128)S(1)}, s32[128]{0:T(128)}, u32[]{:S(2)}) copy-start(s32[128]{0:T(128)} %param.11) | copy-start | bytes 1540
  96.2 19.0 %all-to-all-start = ((f32[4,32,2048]{2,1,0:T(8,128)}), f32[4,32,2048]{2,1,0:T(8,128)S(1)}, u32[]{:S(2)}, u32[]{:S(2)}) async-start(f32[4,32,2048]{2,1,0:T(8,128)} %bitcast.308), calls=%async_computation | async-start | bytes 2097152 | tf_op jit(solution)/shard_map/all_to_all | solution.py:56
where the time goes:
time: 140 us; the launch traced here: 139 us
  blocking collectives  61.7 us (44%)
  other arithmetic  30.3 us (22%)
  matrix products  24.1 us (17%)
  starting transfers between devices  9.24 us (7%)
  waiting for transfers between devices  7.19 us (5%)
  local copies, waits for them, and re-layouts  5.66 us (4%)
    all_gather x3, blocking collectives, gathered_once(): both, at, found = (lax.all_gather(jnp.concatenate(lines), axis), 0, {})  43.7 us
    dot_general x1, matrix products, local(): jnp.einsum('qhd,kd->hqk', query_latent, key_latent, preferred_element_typ...  19.6 us
    all_to_all x1, blocking collectives, from_everyone(): return lax.all_to_all(copies, axis, split_axis=0, concat_axis=0, tiled=True)  18 us
    reduce_sum x1, other arithmetic, local(): jnp.sum(jnp.where(allowed[None], jnp.exp(scores - local_top[:, :, None]),...  14.3 us
    all_to_all x1, waiting for transfers between devices, sum_at_owner(): lax.all_to_all(cut_along(shard, dim, count), axis, 0, 0, tiled=True)  7.19 us
    reduce_sum x1, other arithmetic, local(): head_part = jnp.sum(weights, axis=0)  7.02 us
    all_to_all x1, starting transfers between devices, side_by_side(): lax.all_to_all(both, axis, split_axis=split_dim, concat_axis=concat_dim,...  4.83 us
    dot_general x1, matrix products, local(): jnp.einsum('qjd,kd->qjk', index_query, index_key, preferred_element_type=...  4.43 us
  transfers between devices with their start and end apart: 2, of which 1 were waited for; matrix products, arithmetic and copies ran while one was open for 36% of the time, Pallas kernels for 0%

commit v1 on v0

v1 whole, which is shorter than its diff:
```python
import jax
import jax.numpy as jnp
from jax import lax
from jax.experimental import pallas as pl
from jax.experimental.pallas import tpu as pltpu
from jax.sharding import Mesh
from jax.sharding import PartitionSpec as P

H = 128
CTX = ("z", "y", "c")
NEG = -1e30
MESH = pl.DeviceIdType.MESH
f32 = jnp.float32
KL = 2048
NE = 6


def lane_swap(a, b, keep, shift):
    return (
        jnp.where(keep, a, pltpu.roll(b, shift, 1)),
        jnp.where(keep, pltpu.roll(a, 128 - shift, 1), b),
    )


def lane_groups(shape):
    lane = lax.broadcasted_iota(jnp.int32, shape, 1)
    return (lane // 8) % 2 == 0, (lane // 16) % 2 == 0


def build_weights(q_ref, w_ref, i):
    even, low = lane_groups((576, 128))
    a = [q_ref[4 * i + g] for g in range(4)]
    a[0], a[1] = lane_swap(a[0], a[1], even, 8)
    a[2], a[3] = lane_swap(a[2], a[3], even, 8)
    a[0], a[2] = lane_swap(a[0], a[2], low, 16)
    a[1], a[3] = lane_swap(a[1], a[3], low, 16)
    for c in range(4):
        w_ref[c, :, pl.ds(pl.multiple_of(i * 128, 128), 128)] = a[c]


def dot_into(s_ref, k_ref, w_ref, t):
    w = w_ref[t // 4, :, pl.ds(pl.multiple_of((t % 4) * 256, 256), 256)]
    s_ref[...] = lax.dot_general(
        k_ref[...], w, (((1,), (0,)), ((), ())), preferred_element_type=f32
    )


def exp_from(s_ref, e_ref, top_ref, sum_ref, thr_ref, t):
    th = thr_ref[t // 4]
    acc = [[None] * 4 for _ in range(2)]
    for k in range(KL // 8):
        m = th >= 8 * k
        for j in range(2):
            v = jnp.where(m, s_ref[8 * k : 8 * k + 8, j * 128 : (j + 1) * 128], NEG)
            a = k % 4
            acc[j][a] = v if acc[j][a] is None else jnp.maximum(acc[j][a], v)
    tops = []
    for j in range(2):
        m = jnp.maximum(
            jnp.maximum(acc[j][0], acc[j][1]), jnp.maximum(acc[j][2], acc[j][3])
        )
        m = jnp.max(m, axis=0, keepdims=True)
        top_ref[pl.ds(2 * t + j, 1), :] = m
        tops.append(jnp.broadcast_to(m, (8, 128)))
    acc = [[None] * 4 for _ in range(2)]
    for k in range(KL // 8):
        m = th >= 8 * k
        for j in range(2):
            s = s_ref[8 * k : 8 * k + 8, j * 128 : (j + 1) * 128]
            v = jnp.where(m, jnp.exp(s - tops[j]), 0.0)
            e_ref[2 * t + j, 8 * k : 8 * k + 8, :] = v
            a = k % 4
            acc[j][a] = v if acc[j][a] is None else acc[j][a] + v
    for j in range(2):
        m = (acc[j][0] + acc[j][1]) + (acc[j][2] + acc[j][3])
        sum_ref[pl.ds(2 * t + j, 1), :] = jnp.sum(m, axis=0, keepdims=True)


def lse_of(top, total):
    some = total > 0
    return jnp.where(some, top + jnp.log(jnp.where(some, total, 1.0)), NEG)


def merge_lse(v):
    m = jnp.max(v, axis=0)
    return m + jnp.log(jnp.sum(jnp.exp(v - m[None]), axis=0))


def as_row(column):
    n = column.shape[0]
    row = lax.broadcasted_iota(jnp.int32, (n, 128), 0)
    lane = lax.broadcasted_iota(jnp.int32, (n, 128), 1)
    return jnp.sum(jnp.where(row == lane, column, 0.0), axis=0, keepdims=True)


def kernel(
    pos_s, pos_v, q_hbm, k_hbm, iq_hbm, iw_hbm, ik_hbm,
    tgt_ref, div_ref,
    q_ref, kt_ref, k_ref, w_ref, s0_ref, s1_ref, e_ref, top_ref, sum_ref, thr_ref,
    iq_ref, iw_ref, ik_ref, wc_ref, lg_ref, u_ref, part_ref, got_ref,
    ab_ref, bb_ref, l_ref, pc_ref, cm_ref,
    in_sem, ix_sem, ix_send, ix_recv, a_send, a_recv, b_send, b_recv, r_send, r_recv,
):
    z, y, c0, x = (lax.axis_index(n) for n in ("z", "y", "c", "x"))
    me_a = y * 2 + c0
    base = ((z * 4 + y) * 2 + c0) * KL

    def x_peer(d):
        return {"z": z, "y": y, "c": c0, "x": lax.rem(x + d, 4)}

    def a_peer(d):
        p = lax.rem(me_a + d, 8)
        return {"z": z, "y": p // 2, "c": lax.rem(p, 2), "x": x}

    def b_peer(d):
        return {"z": lax.rem(z + d, 8), "y": y, "c": c0, "x": x}

    copies = [
        pltpu.make_async_copy(k_hbm, kt_ref, in_sem.at[0]),
        pltpu.make_async_copy(q_hbm.at[pl.ds(0, 16)], q_ref.at[pl.ds(0, 16)], in_sem.at[1]),
        pltpu.make_async_copy(q_hbm.at[pl.ds(16, 16)], q_ref.at[pl.ds(16, 16)], in_sem.at[2]),
        pltpu.make_async_copy(ik_hbm, ik_ref, in_sem.at[3]),
    ]
    for cp in copies:
        cp.start()
    own_iq = pltpu.make_async_copy(
        iq_hbm.at[pl.ds(pl.multiple_of(x * 32, 32), 32)], iq_ref.at[x], ix_sem.at[0]
    )
    own_iw = pltpu.make_async_copy(iw_hbm, iw_ref.at[x], ix_sem.at[1])
    own_iq.start()
    own_iw.start()

    barrier = pltpu.get_barrier_semaphore()
    for d in range(1, 4):
        pl.semaphore_signal(barrier, inc=1, device_id=x_peer(d), device_id_type=MESH)
    for d in range(1, 8):
        pl.semaphore_signal(barrier, inc=1, device_id=a_peer(d), device_id_type=MESH)
        pl.semaphore_signal(barrier, inc=1, device_id=b_peer(d), device_id_type=MESH)

    group = (lax.broadcasted_iota(jnp.int32, (8, 128), 1) // 8) % 4
    sub = lax.broadcasted_iota(jnp.int32, (8, 128), 0)
    pos8 = jnp.broadcast_to(pos_v[...], (8, 128))
    for c in range(4):
        th = pos8
        for g in range(4):
            if g != c:
                th = jnp.where(group == g, pltpu.roll(pos8, (8 * (g - c)) % 128, 1), th)
        thr_ref[c] = th - base - sub
    for q in range(32):
        pc_ref[q : q + 1, :] = jnp.full((1, 128), pos_s[x * 32 + q] - base, jnp.int32)

    copies[0].wait()
    for n in range(KL // 128):
        k_ref[n * 128 : (n + 1) * 128, :] = kt_ref[:, n * 128 : (n + 1) * 128].T
    copies[1].wait()
    copies[2].wait()

    @pl.loop(0, 8)
    def _(i):
        build_weights(q_ref, w_ref, i)

    dot_into(s0_ref, k_ref, w_ref, 0)

    pl.semaphore_wait(barrier, 17)
    own_iq.wait()
    own_iw.wait()

    def ix_copies(d):
        peer = x_peer(d)
        to = lax.rem(x + d, 4)
        return [
            pltpu.make_async_remote_copy(
                iq_hbm.at[pl.ds(pl.multiple_of(to * 32, 32), 32)], iq_ref.at[x],
                ix_send.at[0], ix_recv.at[0], device_id=peer, device_id_type=MESH,
            ),
            pltpu.make_async_remote_copy(
                iw_hbm, iw_ref.at[x],
                ix_send.at[1], ix_recv.at[1], device_id=peer, device_id_type=MESH,
            ),
        ]

    for d in range(1, 4):
        for cp in ix_copies(d):
            cp.start()

    def exchange_start(buf, me, e, value, send, recv, peer):
        buf[e, me] = value
        for d in range(1, 8):
            pltpu.make_async_remote_copy(
                buf.at[e, me], buf.at[e, me], send.at[e], recv.at[e],
                device_id=peer(d), device_id_type=MESH,
            ).start()

    def seven(buf, e, send, recv):
        return pltpu.make_async_remote_copy(
            buf.at[e, pl.ds(0, 7)], buf.at[e, pl.ds(0, 7)], send.at[e], recv.at[e],
            device_id=x_peer(1), device_id_type=MESH,
        )

    def a_start(e, value):
        exchange_start(ab_ref, me_a, e, value, a_send, a_recv, a_peer)

    def a_done(e):
        seven(ab_ref, e, a_send, a_recv).wait_recv()
        return ab_ref[e]

    def b_start(e, value):
        exchange_start(bb_ref, z, e, value, b_send, b_recv, b_peer)

    def b_done(e):
        seven(bb_ref, e, b_send, b_recv).wait_recv()
        return bb_ref[e]

    def stats_out(c):
        rows = pl.ds(pl.multiple_of(c * 8, 8), 8)
        a_start(c, lse_of(top_ref[rows, :], sum_ref[rows, :]))

    def middle(c):
        b_start(c, merge_lse(a_done(c)))

    def head_sum(c):
        lse = merge_lse(b_done(c))
        rows = pl.ds(pl.multiple_of(c * 8, 8), 8)
        l_ref[...] = jnp.exp(top_ref[rows, :] - lse) * (1.0 / H)
        coef = [jnp.broadcast_to(l_ref[i : i + 1, :], (8, 128)) for i in range(8)]
        even, low = lane_groups((8, 128))

        def pair(a, b, keep, shift):
            other = jnp.where(keep, b, a)
            return jnp.where(keep, a, b) + jnp.where(
                keep, pltpu.roll(other, 128 - shift, 1), pltpu.roll(other, shift, 1)
            )

        @pl.loop(0, 8)
        def _(kb):
            for k in range(8):
                acc = []
                for g in range(4):
                    at = pl.ds(pl.multiple_of(g * 512 + kb * 64, 64) + k * 8, 8)
                    s = e_ref[c * 8, at, :] * coef[0]
                    for i in range(1, 8):
                        s = s + e_ref[c * 8 + i, at, :] * coef[i]
                    acc.append(s)
                u_ref[pl.ds(pl.multiple_of(kb * 64, 64) + k * 8, 8), :] = pair(
                    pair(acc[0], acc[1], even, 8), pair(acc[2], acc[3], even, 8), low, 16
                )

        for n in range(4):
            part_ref[c, :, n * 128 : (n + 1) * 128] = u_ref[n * 128 : (n + 1) * 128, :].T
        for d in range(1, 4):
            to = lax.rem(x + d, 4)
            pltpu.make_async_remote_copy(
                part_ref.at[c, pl.ds(pl.multiple_of(to * 32, 32), 32)], got_ref.at[c, x],
                r_send.at[c], r_recv.at[c], device_id=x_peer(d), device_id_type=MESH,
            ).start()

    def three(c):
        return pltpu.make_async_remote_copy(
            got_ref.at[c, pl.ds(0, 3)], got_ref.at[c, pl.ds(0, 3)],
            r_send.at[c], r_recv.at[c], device_id=x_peer(1), device_id_type=MESH,
        )

    def own_rows(c):
        three(c).wait_recv()
        got_ref[c, x] = part_ref[c, pl.ds(pl.multiple_of(x * 32, 32), 32)]
        cross = mass = None
        for g in range(4):
            t = got_ref[c, 0, 8 * g : 8 * g + 8]
            for k in range(1, 4):
                t = t + got_ref[c, k, 8 * g : 8 * g + 8]
            lg = lg_ref[8 * c : 8 * c + 8, g * 512 : (g + 1) * 512]
            tgt_ref[8 * c : 8 * c + 8, g * 512 : (g + 1) * 512] = t
            positive = t > 0
            term = jnp.where(positive, t * jnp.log(jnp.where(positive, t, 1.0)), 0.0) - t * lg
            cross = term if cross is None else cross + term
            mass = t if mass is None else mass + t
        cm_ref[0, 8 * c : 8 * c + 8, :] = jnp.broadcast_to(
            jnp.sum(cross, axis=1, keepdims=True), (8, 128)
        )
        cm_ref[1, 8 * c : 8 * c + 8, :] = jnp.broadcast_to(
            jnp.sum(mass, axis=1, keepdims=True), (8, 128)
        )

    @pl.loop(0, 4)
    def _(c):
        @pl.loop(0, 2)
        def _(h):
            t = c * 4 + h * 2
            dot_into(s1_ref, k_ref, w_ref, t + 1)
            exp_from(s0_ref, e_ref, top_ref, sum_ref, thr_ref, t)
            dot_into(s0_ref, k_ref, w_ref, jnp.minimum(t + 2, 15))
            exp_from(s1_ref, e_ref, top_ref, sum_ref, thr_ref, t + 1)

        stats_out(c)

        @pl.when(c >= 1)
        def _():
            middle(c - 1)

        @pl.when(c >= 2)
        def _():
            head_sum(c - 2)

    for k in range(2):
        n = (3 * 32, 3)[k]
        ref = (iq_ref, iw_ref)[k]
        pltpu.make_async_remote_copy(
            ref.at[pl.ds(0, 3)], ref.at[pl.ds(0, 3)], ix_send.at[k], ix_recv.at[k],
            device_id=x_peer(1), device_id_type=MESH,
        ).wait_recv()
    copies[3].wait()
    for k in range(4):
        w = pltpu.roll(iw_ref[k].astype(f32), lax.rem(128 - 32 * x, 128), 1)
        for q in range(32):
            wc_ref[k * 512 + q * 16 : k * 512 + q * 16 + 16, :] = jnp.broadcast_to(
                w[:, q : q + 1], (16, 128)
            )

    def logits_block(n):
        keys = ik_ref[pl.ds(pl.multiple_of(n * 256, 256), 256), :]
        s0_ref[...] = lax.dot_general(
            iq_ref[...].reshape(2048, 128), keys, (((1,), (1,)), ((), ())),
            preferred_element_type=f32,
        )
        for q in range(32):
            acc = [None, None]
            for k in range(4):
                for h in range(2):
                    r = k * 512 + q * 16 + h * 8
                    w = wc_ref[r : r + 8, :]
                    for j in range(2):
                        v = w * jnp.maximum(s0_ref[r : r + 8, j * 128 : (j + 1) * 128], 0.0)
                        acc[j] = v if acc[j] is None else acc[j] + v
            for j in range(2):
                lg_ref[q : q + 1, pl.ds(pl.multiple_of(n * 256 + j * 128, 128), 128)] = jnp.sum(
                    acc[j], axis=0, keepdims=True
                )

    @pl.loop(0, 4)
    def _(n):
        logits_block(n)

    middle(3)

    @pl.loop(4, 8)
    def _(n):
        logits_block(n)

    head_sum(2)

    cols = []
    lane = lax.broadcasted_iota(jnp.int32, (8, KL), 1)
    for c in range(4):
        rows = slice(8 * c, 8 * c + 8)
        ok = lane <= jnp.broadcast_to(pc_ref[rows, 0:1], (8, KL))
        v = jnp.where(ok, lg_ref[rows, :], NEG)
        top = jnp.max(v, axis=1, keepdims=True)
        total = jnp.sum(jnp.where(ok, jnp.exp(v - top), 0.0), axis=1, keepdims=True)
        cols.append(lse_of(top, total))
    a_start(4, jnp.broadcast_to(as_row(jnp.concatenate(cols, axis=0)), (8, 128)))

    head_sum(3)
    middle(4)
    for c in range(4):
        own_rows(c)
    spread = merge_lse(b_done(4))
    value = as_row(cm_ref[0]) + spread * as_row(cm_ref[1])
    a_start(5, value)
    b_start(5, jnp.sum(a_done(5), axis=0))
    div_ref[...] = jnp.sum(b_done(5), axis=0)

    for k in range(2):
        ref = (iq_ref, iw_ref)[k]
        pltpu.make_async_remote_copy(
            ref.at[pl.ds(0, 3)], ref.at[pl.ds(0, 3)], ix_send.at[k], ix_recv.at[k],
            device_id=x_peer(1), device_id_type=MESH,
        ).wait_send()
    for e in range(NE):
        seven(ab_ref, e, a_send, a_recv).wait_send()
        seven(bb_ref, e, b_send, b_recv).wait_send()
    for c in range(4):
        three(c).wait_send()


def local(query_latent, key_latent, index_query, index_weight, index_key, positions):
    vmem = pl.BlockSpec(memory_space=pltpu.VMEM)
    hbm = pl.BlockSpec(memory_space=pl.ANY)
    bf16 = jnp.bfloat16
    dma = pltpu.SemaphoreType.DMA
    target, divergence = pl.pallas_call(
        kernel,
        out_shape=(
            jax.ShapeDtypeStruct((32, KL), f32),
            jax.ShapeDtypeStruct((8, 128), f32),
        ),
        in_specs=[pl.BlockSpec(memory_space=pltpu.SMEM), vmem, hbm, hbm, hbm, hbm, hbm],
        out_specs=(vmem, vmem),
        scratch_shapes=[
            pltpu.VMEM((32, 576, 128), bf16),
            pltpu.VMEM((576, KL), bf16),
            pltpu.VMEM((KL, 576), bf16),
            pltpu.VMEM((4, 576, 1024), bf16),
            pltpu.VMEM((KL, 256), f32),
            pltpu.VMEM((KL, 256), f32),
            pltpu.VMEM((32, KL, 128), f32),
            pltpu.VMEM((32, 128), f32),
            pltpu.VMEM((32, 128), f32),
            pltpu.VMEM((4, 8, 128), jnp.int32),
            pltpu.VMEM((4, 32, 16, 128), bf16),
            pltpu.VMEM((4, 16, 128), bf16),
            pltpu.VMEM((KL, 128), bf16),
            pltpu.VMEM((2048, 128), f32),
            pltpu.VMEM((32, KL), f32),
            pltpu.VMEM((512, 128), f32),
            pltpu.VMEM((4, 128, 512), f32),
            pltpu.VMEM((4, 4, 32, 512), f32),
            pltpu.VMEM((NE, 8, 8, 128), f32),
            pltpu.VMEM((NE, 8, 8, 128), f32),
            pltpu.VMEM((8, 128), f32),
            pltpu.VMEM((32, 128), jnp.int32),
            pltpu.VMEM((2, 32, 128), f32),
            dma((4,)), dma((2,)), dma((2,)), dma((2,)),
            dma((NE,)), dma((NE,)), dma((NE,)), dma((NE,)), dma((4,)), dma((4,)),
        ],
        compiler_params=pltpu.CompilerParams(
            collective_id=0, has_side_effects=True, vmem_limit_bytes=66_000_000
        ),
    )(
        positions,
        positions.reshape(1, 128),
        query_latent.transpose(1, 2, 0),
        key_latent.T,
        index_query,
        index_weight.T,
        index_key,
    )
    return target, divergence[0, :32]


def solution(mesh):
    finer = Mesh(
        mesh.devices.reshape(8, 4, 2, mesh.shape["head"]), ("z", "y", "c", "x")
    )
    return jax.shard_map(
        local,
        mesh=finer,
        in_specs=(
            P(None, "x", None),
            P(CTX, None),
            P(None, "x", None),
            P(None, "x"),
            P(CTX, None),
            P(),
        ),
        out_specs=(P("x", CTX), P("x")),
        check_vma=False,
    )
```

time: 140 us -> 68.7 us (0.49)
  Pallas kernels: 0 us -> 65 us
  blocking collectives: 61.7 us -> 0 us
  other arithmetic: 30.3 us -> 0 us
  matrix products: 24.1 us -> 0 us
  starting transfers between devices: 9.24 us -> 0 us
  waiting for transfers between devices: 7.19 us -> 0 us
  local copies, waits for them, and re-layouts: 5.66 us -> 2.86 us
    pallas_call x0 -> x1, Pallas kernels: none -> 65 us  [local(): pl.pallas_call(kernel, out_shape=(jax.ShapeDtypeStruct((32, KL), f32), ja...]
    all_gather x3 -> x0, blocking collectives: 43.7 us -> none  [gathered_once(): both, at, found = (lax.all_gather(jnp.concatenate(lines), axis), 0, {})]
    reduce_sum x4 -> x0, other arithmetic: 24.1 us -> none  [the longest x1 14.3 us: local(): jnp.sum(jnp.where(allowed[None], jnp.exp(scores - local_top[:, :, None]),...]
    dot_general x2 -> x0, matrix products: 24.1 us -> none  [the longest x1 19.6 us: local(): jnp.einsum('qhd,kd->hqk', query_latent, key_latent, preferred_element_typ...]
    all_to_all x1 -> x0, blocking collectives: 18 us -> none  [from_everyone(): return lax.all_to_all(copies, axis, split_axis=0, concat_axis=0, tiled=True)]
    all_to_all x2 -> x0, starting transfers between devices: 9.24 us -> none  [the longest x1 4.83 us: side_by_side(): lax.all_to_all(both, axis, split_axis=split_dim, concat_axis=concat_dim,...]
    all_to_all x2 -> x0, waiting for transfers between devices: 7.19 us -> none  [the longest x1 7.19 us: sum_at_owner(): lax.all_to_all(cut_along(shard, dim, count), axis, 0, 0, tiled=True)]
    concatenate x5 -> x0, other arithmetic: 2.28 us -> none  [the longest x1 2.25 us: side_by_side(): jnp.concatenate([a.reshape(*a.shape[:along], w) for a, w in zip(arrays, w...]
  transfers between devices with their start and end apart: 2 -> 0, of which waited for: 1 -> 0; matrix products, arithmetic and copies ran while one was open for 36% -> 0% of each run, Pallas kernels for 0% -> 0%
where the time goes in v1:
time: 68.7 us; the launch traced here: 68.5 us
  Pallas kernels  65 us (95%)
  local copies, waits for them, and re-layouts  2.86 us (4%)
    pallas_call x1, Pallas kernels, local(): pl.pallas_call(kernel, out_shape=(jax.ShapeDtypeStruct((32, KL), f32), ja...  65 us
    unnamed x1, local copies, waits for them, and re-layouts  1.67 us

profile of v1, /device:TPU:1, one launch (start us, length us, event | category | flops | bytes accessed | tf_op | source)
XLA Modules:
  0.0 68.5 jit_solution(6602319871852647187)
XLA Ops:
  0.6 65.0 %shard_map.77 = (f32[32,2048]{1,0:T(8,128)}, f32[8,128]{1,0:T(8,128)}) custom-call(s32[128]{0:T(128)} %pos_s.1, s32[1,128]{1,0:T(1,128)} %bitcast.9, bf16[32,576,128]{2,1,0:T(8,128)(2,1)} %bitcast.6, bf16[576,2048]{1,0:T(8,128)(2,1)} %bitcast.7, bf16[128,16,128]{2,1,0:T(8,128)(2,1)} %iq_hbm.1, bf16[16,128]{1,0:T(8,128)(2,1)} %bitcast.8, bf16[2048,128]{1,0:T(8,128)(2,1)} %ik_hbm.1), custom_call_target="tpu_custom_call" | custom-call | tf_op jit(solution)/shard_map/pallas_call | solution.py:390
  65.7 1.2 %slice_bitcast_fusion = f32[32]{0:T(128)} fusion(f32[8,128]{1,0:T(8,128)} %get-tuple-element.5), kind=kLoop, calls=%fused_computation | loop fusion | bytes 256 | tf_op jit(solution)/shard_map/squeeze | solution.py:437
  66.9 1.7 %copy.9 = f32[32,2048]{1,0:T(8,128)} copy(f32[32,2048]{1,0:T(8,128)} %get-tuple-element.8) | data formatting | bytes 524288

commit v2 on v1

v2 whole, which is shorter than its diff:
```python
import jax
import jax.numpy as jnp
from jax import lax
from jax.experimental import pallas as pl
from jax.experimental.pallas import tpu as pltpu
from jax.sharding import Mesh
from jax.sharding import PartitionSpec as P

H = 128
CTX = ("z", "y", "c")
NEG = -1e30
MESH = pl.DeviceIdType.MESH
f32 = jnp.float32
KL = 2048
QK = 576
PIECE = 256
NE = 6


def build_weights(q_ref, w_ref, t):
    group = (lax.broadcasted_iota(jnp.int32, (QK, 128), 1) // 8) % 4
    c = t // 4
    for j in range(2):
        i = (t % 4) * 2 + j
        out = None
        for g in range(4):
            r = pltpu.roll(q_ref[4 * i + g], lax.rem(8 * (g - c) + 128, 128), 1)
            out = r if out is None else jnp.where(group == g, r, out)
        w_ref[:, j * 128 : (j + 1) * 128] = out


def score_step(new_ref, old_ref, k_ref, w_ref, e_ref, top_ref, sum_ref, thr_ref, t, new=True,
               old=True, before=None):
    nt = t + 1
    biggest = [[None] * 2 for _ in range(2)]
    total = [[None] * 4 for _ in range(2)]
    if new:
        th = thr_ref[nt // 4]
        w = w_ref[...]
    if old:
        tops = [jnp.broadcast_to(top_ref[pl.ds(2 * t + j, 1), :], (8, 128)) for j in range(2)]
    for p in range(KL // PIECE):
        if before is not None:
            before(p)
        rows = slice(p * PIECE, (p + 1) * PIECE)
        if new:
            r = lax.dot_general(
                k_ref[rows, :], w, (((1,), (0,)), ((), ())), preferred_element_type=f32
            )
            for k in range(PIECE // 8):
                at = p * PIECE + 8 * k
                m = th >= at
                for j in range(2):
                    v = jnp.where(m, r[8 * k : 8 * k + 8, j * 128 : (j + 1) * 128], NEG)
                    new_ref[at : at + 8, j * 128 : (j + 1) * 128] = v
                    a = k % 2
                    biggest[j][a] = v if biggest[j][a] is None else jnp.maximum(biggest[j][a], v)
        if old:
            for k in range(PIECE // 8):
                at = p * PIECE + 8 * k
                for j in range(2):
                    v = jnp.exp(old_ref[at : at + 8, j * 128 : (j + 1) * 128] - tops[j])
                    e_ref[t // 4, at // 8, (t % 4) * 2 + j] = v
                    a = k % 4
                    total[j][a] = v if total[j][a] is None else total[j][a] + v
    for j in range(2):
        if new:
            m = jnp.max(jnp.maximum(biggest[j][0], biggest[j][1]), axis=0, keepdims=True)
            top_ref[pl.ds(2 * nt + j, 1), :] = jnp.maximum(m, 0.5 * NEG)
        if old:
            m = (total[j][0] + total[j][1]) + (total[j][2] + total[j][3])
            sum_ref[pl.ds(2 * t + j, 1), :] = jnp.sum(m, axis=0, keepdims=True)


def lse_of(top, total):
    some = total > 0
    return jnp.where(some, top + jnp.log(jnp.where(some, total, 1.0)), NEG)


def merge_lse(v):
    m = jnp.max(v, axis=0)
    return m + jnp.log(jnp.sum(jnp.exp(v - m[None]), axis=0))


def as_row(column):
    n = column.shape[0]
    row = lax.broadcasted_iota(jnp.int32, (n, 128), 0)
    lane = lax.broadcasted_iota(jnp.int32, (n, 128), 1)
    return jnp.sum(jnp.where(row == lane, column, 0.0), axis=0, keepdims=True)


def kernel(
    pos_s, pos_v, q_hbm, k_hbm, iq_hbm, iw_hbm, ik_hbm,
    tgt_ref, div_ref,
    q_ref, kt_ref, k_ref, w0_ref, w1_ref, s0_ref, s1_ref, e_ref, top_ref, sum_ref, thr_ref,
    iq_ref, iw_ref, ik_ref, wc_ref, lg_ref, u_ref, part_ref, got_ref,
    ab_ref, bb_ref, l_ref, pc_ref, cm_ref, ikt_ref, f_ref,
    in_sem, ix_sem, ix_send, ix_recv, a_send, a_recv, b_send, b_recv, r_send, r_recv,
):
    z, y, c0, x = (lax.axis_index(n) for n in ("z", "y", "c", "x"))
    me_a = y * 2 + c0
    base = ((z * 4 + y) * 2 + c0) * KL

    def x_peer(d):
        return {"z": z, "y": y, "c": c0, "x": lax.rem(x + d, 4)}

    def a_peer(d):
        p = lax.rem(me_a + d, 8)
        return {"z": z, "y": p // 2, "c": lax.rem(p, 2), "x": x}

    def b_peer(d):
        return {"z": lax.rem(z + d, 8), "y": y, "c": c0, "x": x}

    k_in = [
        pltpu.make_async_copy(
            k_hbm.at[:, pl.ds(n * 512, 512)], kt_ref.at[:, pl.ds(n * 512, 512)], in_sem.at[n]
        )
        for n in range(4)
    ]
    q_in = [
        pltpu.make_async_copy(
            q_hbm.at[pl.ds(n * 8, 8)], q_ref.at[pl.ds(n * 8, 8)], in_sem.at[4 + n]
        )
        for n in range(4)
    ]
    ik_in = pltpu.make_async_copy(ik_hbm, ik_ref, in_sem.at[8])
    q_in[0].start()
    for cp in k_in:
        cp.start()
    for cp in q_in[1:]:
        cp.start()
    ik_in.start()
    own_iq = pltpu.make_async_copy(
        iq_hbm.at[pl.ds(x * 4, 4)], iq_ref.at[:, x], ix_sem.at[0]
    )
    own_iw = pltpu.make_async_copy(iw_hbm, iw_ref.at[x], ix_sem.at[1])
    own_iq.start()
    own_iw.start()

    barrier = pltpu.get_barrier_semaphore()
    for d in range(1, 4):
        pl.semaphore_signal(barrier, inc=1, device_id=x_peer(d), device_id_type=MESH)
    for d in range(1, 8):
        pl.semaphore_signal(barrier, inc=1, device_id=a_peer(d), device_id_type=MESH)
        pl.semaphore_signal(barrier, inc=1, device_id=b_peer(d), device_id_type=MESH)

    group = (lax.broadcasted_iota(jnp.int32, (8, 128), 1) // 8) % 4
    sub = lax.broadcasted_iota(jnp.int32, (8, 128), 0)
    pos8 = jnp.broadcast_to(pos_v[...], (8, 128))
    for c in range(4):
        th = pos8
        for g in range(4):
            if g != c:
                th = jnp.where(group == g, pltpu.roll(pos8, (8 * (g - c)) % 128, 1), th)
        thr_ref[c] = th - base - sub
    for q in range(32):
        pc_ref[q : q + 1, :] = jnp.full((1, 128), pos_s[x * 32 + q] - base, jnp.int32)

    q_in[0].wait()
    build_weights(q_ref, w0_ref, 0)

    def key_block(p):
        if p % (512 // PIECE) == 0:
            k_in[p * PIECE // 512].wait()
        for n in range(PIECE // 128):
            at = p * PIECE + n * 128
            k_ref[at : at + 128, :] = kt_ref[:, at : at + 128].T

    score_step(
        s1_ref, s0_ref, k_ref, w0_ref, e_ref, top_ref, sum_ref, thr_ref, -1, old=False,
        before=key_block,
    )
    for cp in q_in[1:]:
        cp.wait()
    build_weights(q_ref, w1_ref, 1)

    pl.semaphore_wait(barrier, 17)
    own_iq.wait()
    own_iw.wait()

    def ix_copies(d):
        peer = x_peer(d)
        to = lax.rem(x + d, 4)
        return [
            pltpu.make_async_remote_copy(
                iq_hbm.at[pl.ds(to * 4, 4)], iq_ref.at[:, x],
                ix_send.at[0], ix_recv.at[0], device_id=peer, device_id_type=MESH,
            ),
            pltpu.make_async_remote_copy(
                iw_hbm, iw_ref.at[x],
                ix_send.at[1], ix_recv.at[1], device_id=peer, device_id_type=MESH,
            ),
        ]

    for d in range(1, 4):
        for cp in ix_copies(d):
            cp.start()

    def ix_all():
        return [
            pltpu.make_async_remote_copy(
                ref, ref, ix_send.at[k], ix_recv.at[k],
                device_id=x_peer(1), device_id_type=MESH,
            )
            for k, ref in enumerate((iq_ref.at[:, pl.ds(0, 3)], iw_ref.at[pl.ds(0, 3)]))
        ]

    def exchange_start(buf, me, e, value, send, recv, peer):
        buf[e, me] = value
        for d in range(1, 8):
            pltpu.make_async_remote_copy(
                buf.at[e, me], buf.at[e, me], send.at[e], recv.at[e],
                device_id=peer(d), device_id_type=MESH,
            ).start()

    def seven(buf, e, send, recv):
        return pltpu.make_async_remote_copy(
            buf.at[e, pl.ds(0, 7)], buf.at[e, pl.ds(0, 7)], send.at[e], recv.at[e],
            device_id=x_peer(1), device_id_type=MESH,
        )

    def a_start(e, value):
        exchange_start(ab_ref, me_a, e, value, a_send, a_recv, a_peer)

    def a_done(e):
        seven(ab_ref, e, a_send, a_recv).wait_recv()
        return ab_ref[e]

    def b_start(e, value):
        exchange_start(bb_ref, z, e, value, b_send, b_recv, b_peer)

    def b_done(e):
        seven(bb_ref, e, b_send, b_recv).wait_recv()
        return bb_ref[e]

    def stats_out(c):
        rows = pl.ds(pl.multiple_of(c * 8, 8), 8)
        a_start(c, lse_of(top_ref[rows, :], sum_ref[rows, :]))

    def middle(c):
        b_start(c, merge_lse(a_done(c)))

    def head_sum(c):
        lse = merge_lse(b_done(c))
        rows = pl.ds(pl.multiple_of(c * 8, 8), 8)
        l_ref[...] = jnp.exp(top_ref[rows, :] - lse) * (1.0 / H)
        coef = [jnp.broadcast_to(l_ref[i : i + 1, :], (8, 128)) for i in range(8)]

        @pl.loop(0, 8)
        def _(b):
            for k in range(32):
                at = b * 32 + k
                s = e_ref[c, at, 0] * coef[0]
                for i in range(1, 8):
                    s = s + e_ref[c, at, i] * coef[i]
                u_ref[at] = s

        for n in range(16):
            v = u_ref[n * 16 : n * 16 + 16].reshape(128, 128).T
            for k in range(4):
                r = [v[32 * k + 8 * g : 32 * k + 8 * g + 8, :] for g in range(4)]
                part_ref[c, k, :, n * 128 : (n + 1) * 128] = (r[0] + r[1]) + (r[2] + r[3])
        for d in range(1, 4):
            to = lax.rem(x + d, 4)
            pltpu.make_async_remote_copy(
                part_ref.at[c, to], got_ref.at[c, x],
                r_send.at[c], r_recv.at[c], device_id=x_peer(d), device_id_type=MESH,
            ).start()

    def three(c):
        return pltpu.make_async_remote_copy(
            got_ref.at[c, pl.ds(0, 3)], got_ref.at[c, pl.ds(0, 3)],
            r_send.at[c], r_recv.at[c], device_id=x_peer(1), device_id_type=MESH,
        )

    def own_rows(c):
        three(c).wait_recv()
        got_ref[c, x] = part_ref[c, x]
        rows = slice(8 * c, 8 * c + 8)
        cross = [None] * 4
        mass = [None] * 4
        for n in range(16):
            at = slice(n * 128, (n + 1) * 128)
            t = (got_ref[c, 0, :, at] + got_ref[c, 1, :, at]) + (
                got_ref[c, 2, :, at] + got_ref[c, 3, :, at]
            )
            tgt_ref[rows, at] = t
            positive = t > 0
            log = jnp.log(jnp.where(positive, t, 1.0))
            term = jnp.where(positive, t * log, 0.0) - t * lg_ref[rows, at]
            a = n % 4
            cross[a] = term if cross[a] is None else cross[a] + term
            mass[a] = t if mass[a] is None else mass[a] + t
        cross = (cross[0] + cross[1]) + (cross[2] + cross[3])
        mass = (mass[0] + mass[1]) + (mass[2] + mass[3])
        cm_ref[0, 8 * c : 8 * c + 8, :] = jnp.broadcast_to(
            jnp.sum(cross, axis=1, keepdims=True), (8, 128)
        )
        cm_ref[1, 8 * c : 8 * c + 8, :] = jnp.broadcast_to(
            jnp.sum(mass, axis=1, keepdims=True), (8, 128)
        )

    @pl.loop(0, 4)
    def _(c):
        @pl.loop(0, 2)
        def _(h):
            t = c * 4 + h * 2
            build_weights(q_ref, w0_ref, jnp.minimum(t + 2, 15))
            score_step(s0_ref, s1_ref, k_ref, w1_ref, e_ref, top_ref, sum_ref, thr_ref, t)

            @pl.when(t < 14)
            def _():
                build_weights(q_ref, w1_ref, jnp.minimum(t + 3, 15))
                score_step(s1_ref, s0_ref, k_ref, w0_ref, e_ref, top_ref, sum_ref, thr_ref, t + 1)

            @pl.when(t == 14)
            def _():
                score_step(
                    s1_ref, s0_ref, k_ref, w0_ref, e_ref, top_ref, sum_ref, thr_ref, t + 1,
                    new=False,
                )

        stats_out(c)

        @pl.when(c >= 1)
        def _():
            middle(c - 1)

        @pl.when(c >= 2)
        def _():
            head_sum(c - 2)

    for cp in ix_all():
        cp.wait_recv()
    ik_in.wait()
    for n in range(KL // 128):
        ikt_ref[:, n * 128 : (n + 1) * 128] = ik_ref[n * 128 : (n + 1) * 128, :].T
    for k in range(4):
        w = pltpu.roll(iw_ref[k].astype(f32), lax.rem(128 - 32 * x, 128), 1)
        for q in range(32):
            wc_ref[q // 8, k, q % 8] = jnp.broadcast_to(w[:, q : q + 1], (16, 128))

    def logits_block(n, s):
        at = pl.ds(pl.multiple_of(n * 256, 256), 256)
        keys = ikt_ref[:, at]
        for b in range(4):
            r = lax.dot_general(
                iq_ref[b].reshape(512, 128), keys, (((1,), (0,)), ((), ())),
                preferred_element_type=f32,
            )
            for q in range(8):
                acc = [None, None]
                for k in range(4):
                    for h in range(2):
                        o = k * 128 + q * 16 + h * 8
                        w = wc_ref[b, k, q, h * 8 : h * 8 + 8, :]
                        for j in range(2):
                            v = w * jnp.maximum(r[o : o + 8, j * 128 : (j + 1) * 128], 0.0)
                            acc[j] = v if acc[j] is None else acc[j] + v
                for j in range(2):
                    f_ref[s, b, j, q * 8 : q * 8 + 8, :] = acc[j]
        for b in range(4):
            for j in range(2):
                v = f_ref[s, b, j, pl.ds(0, 8, stride=8), :]
                for i in range(1, 8):
                    v = v + f_ref[s, b, j, pl.ds(i, 8, stride=8), :]
                lg_ref[8 * b : 8 * b + 8, pl.ds(pl.multiple_of(n * 256 + j * 128, 128), 128)] = v

    @pl.loop(0, 2)
    def _(n):
        logits_block(n * 2, 0)
        logits_block(n * 2 + 1, 1)

    middle(3)

    @pl.loop(2, 4)
    def _(n):
        logits_block(n * 2, 0)
        logits_block(n * 2 + 1, 1)

    head_sum(2)

    cols = []
    lane = lax.broadcasted_iota(jnp.int32, (8, KL), 1)
    for c in range(4):
        rows = slice(8 * c, 8 * c + 8)
        ok = lane <= jnp.broadcast_to(pc_ref[rows, 0:1], (8, KL))
        v = jnp.where(ok, lg_ref[rows, :], NEG)
        top = jnp.max(v, axis=1, keepdims=True)
        total = jnp.sum(jnp.where(ok, jnp.exp(v - top), 0.0), axis=1, keepdims=True)
        cols.append(lse_of(top, total))
    a_start(4, jnp.broadcast_to(as_row(jnp.concatenate(cols, axis=0)), (8, 128)))

    head_sum(3)
    middle(4)
    for c in range(4):
        own_rows(c)
    spread = merge_lse(b_done(4))
    value = as_row(cm_ref[0]) + spread * as_row(cm_ref[1])
    a_start(5, value)
    b_start(5, jnp.sum(a_done(5), axis=0))
    div_ref[...] = jnp.sum(b_done(5), axis=0)

    for cp in ix_all():
        cp.wait_send()
    for e in range(NE):
        seven(ab_ref, e, a_send, a_recv).wait_send()
        seven(bb_ref, e, b_send, b_recv).wait_send()
    for c in range(4):
        three(c).wait_send()


def local(query_latent, key_latent, index_query, index_weight, index_key, positions):
    vmem = pl.BlockSpec(memory_space=pltpu.VMEM)
    hbm = pl.BlockSpec(memory_space=pl.ANY)
    bf16 = jnp.bfloat16
    dma = pltpu.SemaphoreType.DMA
    target, divergence = pl.pallas_call(
        kernel,
        out_shape=(
            jax.ShapeDtypeStruct((32, KL), f32),
            jax.ShapeDtypeStruct((8, 128), f32),
        ),
        in_specs=[pl.BlockSpec(memory_space=pltpu.SMEM), vmem, hbm, hbm, hbm, hbm, hbm],
        out_specs=(vmem, vmem),
        scratch_shapes=[
            pltpu.VMEM((32, 576, 128), bf16),
            pltpu.VMEM((576, KL), bf16),
            pltpu.VMEM((KL, 576), bf16),
            pltpu.VMEM((QK, 256), bf16),
            pltpu.VMEM((QK, 256), bf16),
            pltpu.VMEM((KL, 256), f32),
            pltpu.VMEM((KL, 256), f32),
            pltpu.VMEM((4, KL // 8, 8, 8, 128), f32),
            pltpu.VMEM((32, 128), f32),
            pltpu.VMEM((32, 128), f32),
            pltpu.VMEM((4, 8, 128), jnp.int32),
            pltpu.VMEM((4, 4, 8, 16, 128), bf16),
            pltpu.VMEM((4, 16, 128), bf16),
            pltpu.VMEM((KL, 128), bf16),
            pltpu.VMEM((4, 4, 8, 16, 128), f32),
            pltpu.VMEM((32, KL), f32),
            pltpu.VMEM((KL // 8, 8, 128), f32),
            pltpu.VMEM((4, 4, 8, KL), f32),
            pltpu.VMEM((4, 4, 8, KL), f32),
            pltpu.VMEM((NE, 8, 8, 128), f32),
            pltpu.VMEM((NE, 8, 8, 128), f32),
            pltpu.VMEM((8, 128), f32),
            pltpu.VMEM((32, 128), jnp.int32),
            pltpu.VMEM((2, 32, 128), f32),
            pltpu.VMEM((128, KL), bf16),
            pltpu.VMEM((2, 4, 2, 64, 128), f32),
            dma((9,)), dma((2,)), dma((2,)), dma((2,)),
            dma((NE,)), dma((NE,)), dma((NE,)), dma((NE,)), dma((4,)), dma((4,)),
        ],
        compiler_params=pltpu.CompilerParams(
            collective_id=0, has_side_effects=True, vmem_limit_bytes=66_000_000
        ),
    )(
        positions,
        positions.reshape(1, 128),
        query_latent.transpose(1, 2, 0),
        key_latent.T,
        index_query.reshape(16, 8, 16, 128),
        index_weight.T,
        index_key,
    )
    return target, divergence[0, :32]


def solution(mesh):
    finer = Mesh(
        mesh.devices.reshape(8, 4, 2, mesh.shape["head"]), ("z", "y", "c", "x")
    )
    return jax.shard_map(
        local,
        mesh=finer,
        in_specs=(
            P(None, "x", None),
            P(CTX, None),
            P(None, "x", None),
            P(None, "x"),
            P(CTX, None),
            P(),
        ),
        out_specs=(P("x", CTX), P("x")),
        check_vma=False,
    )
```

time: 68.7 us -> 56.9 us (0.83)
  Pallas kernels: 65 us -> 53.2 us
    pallas_call x1, Pallas kernels: 65 us -> 53.2 us  [local(): pl.pallas_call(kernel, out_shape=(jax.ShapeDtypeStruct((32, KL), f32), ja...]
where the time goes in v2:
time: 56.9 us; the launch traced here: 56.7 us
  Pallas kernels  53.2 us (93%)
  local copies, waits for them, and re-layouts  2.86 us (5%)
  between operations  0.64 us (1%)
    pallas_call x1, Pallas kernels, local(): pl.pallas_call(kernel, out_shape=(jax.ShapeDtypeStruct((32, KL), f32), ja...  53.2 us
    unnamed x1, local copies, waits for them, and re-layouts  1.67 us
    squeeze x1, local copies, waits for them, and re-layouts, local(): return (target, divergence[0, :32])  1.2 us

profile of v2, /device:TPU:1, one launch (start us, length us, event | category | flops | bytes accessed | tf_op | source)
XLA Modules:
  0.0 56.7 jit_solution(7835774019207220121)
XLA Ops:
  0.6 53.2 %shard_map.77 = (f32[32,2048]{1,0:T(8,128)}, f32[8,128]{1,0:T(8,128)}) custom-call(s32[128]{0:T(128)} %pos_s.1, s32[1,128]{1,0:T(1,128)} %bitcast.11, bf16[32,576,128]{2,1,0:T(8,128)(2,1)} %bitcast.7, bf16[576,2048]{1,0:T(8,128)(2,1)} %bitcast.8, bf16[16,8,16,128]{3,2,1,0:T(8,128)(2,1)} %bitcast.9, bf16[16,128]{1,0:T(8,128)(2,1)} %bitcast.10, ...), custom_call_target="tpu_custom_call" | custom-call | tf_op jit(solution)/shard_map/pallas_call | solution.py:418
  53.9 1.2 %slice_bitcast_fusion = f32[32]{0:T(128)} fusion(f32[8,128]{1,0:T(8,128)} %get-tuple-element.5), kind=kLoop, calls=%fused_computation | loop fusion | bytes 256 | tf_op jit(solution)/shard_map/squeeze | solution.py:468
  55.1 1.7 %copy.9 = f32[32,2048]{1,0:T(8,128)} copy(f32[32,2048]{1,0:T(8,128)} %get-tuple-element.8) | data formatting | bytes 524288

commit v3 on v2

--- a/solution.py
+++ b/solution.py
@@ -1,3 +1,5 @@
+import functools
+
 import jax
 import jax.numpy as jnp
 from jax import lax
@@ -32,8 +34,8 @@
 def score_step(new_ref, old_ref, k_ref, w_ref, e_ref, top_ref, sum_ref, thr_ref, t, new=True,
                old=True, before=None):
     nt = t + 1
-    biggest = [[None] * 2 for _ in range(2)]
-    total = [[None] * 4 for _ in range(2)]
+    biggest = [[None] * 8 for _ in range(2)]
+    total = [None] * 2
     if new:
         th = thr_ref[nt // 4]
         w = w_ref[...]
@@ -53,7 +55,7 @@
                 for j in range(2):
                     v = jnp.where(m, r[8 * k : 8 * k + 8, j * 128 : (j + 1) * 128], NEG)
                     new_ref[at : at + 8, j * 128 : (j + 1) * 128] = v
-                    a = k % 2
+                    a = k % 8
                     biggest[j][a] = v if biggest[j][a] is None else jnp.maximum(biggest[j][a], v)
         if old:
             for k in range(PIECE // 8):
@@ -61,15 +63,13 @@
                 for j in range(2):
                     v = jnp.exp(old_ref[at : at + 8, j * 128 : (j + 1) * 128] - tops[j])
                     e_ref[t // 4, at // 8, (t % 4) * 2 + j] = v
-                    a = k % 4
-                    total[j][a] = v if total[j][a] is None else total[j][a] + v
+                    total[j] = v if total[j] is None else total[j] + v
     for j in range(2):
         if new:
-            m = jnp.max(jnp.maximum(biggest[j][0], biggest[j][1]), axis=0, keepdims=True)
+            m = jnp.max(functools.reduce(jnp.maximum, biggest[j]), axis=0, keepdims=True)
             top_ref[pl.ds(2 * nt + j, 1), :] = jnp.maximum(m, 0.5 * NEG)
         if old:
-            m = (total[j][0] + total[j][1]) + (total[j][2] + total[j][3])
-            sum_ref[pl.ds(2 * t + j, 1), :] = jnp.sum(m, axis=0, keepdims=True)
+            sum_ref[pl.ds(2 * t + j, 1), :] = jnp.sum(total[j], axis=0, keepdims=True)
 
 
 def lse_of(top, total):
@@ -127,9 +127,6 @@
     q_in[0].start()
     for cp in k_in:
         cp.start()
-    for cp in q_in[1:]:
-        cp.start()
-    ik_in.start()
     own_iq = pltpu.make_async_copy(
         iq_hbm.at[pl.ds(x * 4, 4)], iq_ref.at[:, x], ix_sem.at[0]
     )
@@ -162,6 +159,10 @@
     def key_block(p):
         if p % (512 // PIECE) == 0:
             k_in[p * PIECE // 512].wait()
+        if p == 0:
+            for cp in q_in[1:]:
+                cp.start()
+            ik_in.start()
         for n in range(PIECE // 128):
             at = p * PIECE + n * 128
             k_ref[at : at + 128, :] = kt_ref[:, at : at + 128].T
@@ -326,9 +327,8 @@
         def _():
             middle(c - 1)
 
-        @pl.when(c >= 2)
-        def _():
-            head_sum(c - 2)
+    head_sum(0)
+    head_sum(1)
 
     for cp in ix_all():
         cp.wait_recv()
@@ -391,9 +391,10 @@
         cols.append(lse_of(top, total))
     a_start(4, jnp.broadcast_to(as_row(jnp.concatenate(cols, axis=0)), (8, 128)))
 
+    own_rows(0)
     head_sum(3)
     middle(4)
-    for c in range(4):
+    for c in range(1, 4):
         own_rows(c)
     spread = merge_lse(b_done(4))
     value = as_row(cm_ref[0]) + spread * as_row(cm_ref[1])
@@ -408,6 +409,11 @@
         seven(bb_ref, e, b_send, b_recv).wait_send()
     for c in range(4):
         three(c).wait_send()
+
+
+def results(sum_ref, row_ref, tgt_ref, div_ref):
+    tgt_ref[...] = sum_ref[...]
+    div_ref[...] = row_ref[0, 0:32]
 
 
 def local(query_latent, key_latent, index_query, index_weight, index_key, positions):
@@ -454,7 +460,7 @@
             dma((NE,)), dma((NE,)), dma((NE,)), dma((NE,)), dma((4,)), dma((4,)),
         ],
         compiler_params=pltpu.CompilerParams(
-            collective_id=0, has_side_effects=True, vmem_limit_bytes=66_000_000
+            collective_id=0, has_side_effects=True, vmem_limit_bytes=58_000_000
         ),
     )(
         positions,
@@ -465,7 +471,16 @@
         index_weight.T,
         index_key,
     )
-    return target, divergence[0, :32]
+    return pl.pallas_call(
+        results,
+        out_shape=(
+            jax.ShapeDtypeStruct((32, KL), f32),
+            jax.ShapeDtypeStruct((32,), f32),
+        ),
+        in_specs=[vmem, vmem],
+        out_specs=(vmem, vmem),
+        compiler_params=pltpu.CompilerParams(vmem_limit_bytes=66_000_000),
+    )(target, divergence)
 
 
 def solution(mesh):

time: 56.9 us -> 55.2 us (0.970)
  local copies, waits for them, and re-layouts: 2.86 us -> 0 us
  Pallas kernels: 53.2 us -> 54.4 us
    pallas_call x0 -> x1, Pallas kernels: none -> 1.68 us  [local(): pl.pallas_call(results, out_shape=(jax.ShapeDtypeStruct((32, KL), f32), j...]
    unnamed x1 -> x0, local copies, waits for them, and re-layouts: 1.67 us -> none
    squeeze x1 -> x0, local copies, waits for them, and re-layouts: 1.2 us -> none  [local(): return (target, divergence[0, :32])]
where the time goes in v3:
time: 55.2 us; the launch traced here: 55 us
  Pallas kernels  54.4 us (99%)
  between operations  0.64 us (1%)
    pallas_call x1, Pallas kernels, local(): pl.pallas_call(kernel, out_shape=(jax.ShapeDtypeStruct((32, KL), f32), ja...  52.7 us
    pallas_call x1, Pallas kernels, local(): pl.pallas_call(results, out_shape=(jax.ShapeDtypeStruct((32, KL), f32), j...  1.68 us

profile of v3, /device:TPU:1, one launch (start us, length us, event | category | flops | bytes accessed | tf_op | source)
XLA Modules:
  0.0 55.0 jit_solution(7679271398885463992)
XLA Ops:
  0.6 52.7 %shard_map.77 = (f32[32,2048]{1,0:T(8,128)}, f32[8,128]{1,0:T(8,128)}) custom-call(s32[128]{0:T(128)} %pos_s.1, s32[1,128]{1,0:T(1,128)} %bitcast.9, bf16[32,576,128]{2,1,0:T(8,128)(2,1)} %bitcast.5, bf16[576,2048]{1,0:T(8,128)(2,1)} %bitcast.6, bf16[16,8,16,128]{3,2,1,0:T(8,128)(2,1)} %bitcast.7, bf16[16,128]{1,0:T(8,128)(2,1)} %bitcast.8, ...), custom_call_target="tpu_custom_call" | custom-call | tf_op jit(solution)/shard_map/pallas_call | solution.py:424
  53.4 1.7 %shard_map.78 = (f32[32,2048]{1,0:T(8,128)}, f32[32]{0:T(128)}) custom-call(f32[32,2048]{1,0:T(8,128)} %get-tuple-element.4.sum_ref, f32[8,128]{1,0:T(8,128)} %get-tuple-element.5.row_ref), custom_call_target="tpu_custom_call" | custom-call | tf_op jit(solution)/shard_map/pallas_call | solution.py:474

commit v4 on v3

--- a/solution.py
+++ b/solution.py
@@ -16,7 +16,7 @@
 KL = 2048
 QK = 576
 PIECE = 256
-NE = 6
+NE = 5
 
 
 def build_weights(q_ref, w_ref, t):
@@ -94,8 +94,8 @@
     tgt_ref, div_ref,
     q_ref, kt_ref, k_ref, w0_ref, w1_ref, s0_ref, s1_ref, e_ref, top_ref, sum_ref, thr_ref,
     iq_ref, iw_ref, ik_ref, wc_ref, lg_ref, u_ref, part_ref, got_ref,
-    ab_ref, bb_ref, l_ref, pc_ref, cm_ref, ikt_ref, f_ref,
-    in_sem, ix_sem, ix_send, ix_recv, a_send, a_recv, b_send, b_recv, r_send, r_recv,
+    ab_ref, bb_ref, l_ref, pc_ref, cm_ref, ikt_ref, f_ref, fin_ref,
+    in_sem, ix_sem, ix_send, ix_recv, a_send, a_recv, b_send, b_recv, r_send, r_recv, f_send, f_recv,
 ):
     z, y, c0, x = (lax.axis_index(n) for n in ("z", "y", "c", "x"))
     me_a = y * 2 + c0
@@ -110,6 +110,12 @@
 
     def b_peer(d):
         return {"z": lax.rem(z + d, 8), "y": y, "c": c0, "x": x}
+
+    me_c = (z * 4 + y) * 2 + c0
+
+    def c_peer(d):
+        p = lax.rem(me_c + d, 64)
+        return {"z": p // 8, "y": lax.rem(p // 2, 4), "c": lax.rem(p, 2), "x": x}
 
     k_in = [
         pltpu.make_async_copy(
@@ -137,9 +143,8 @@
     barrier = pltpu.get_barrier_semaphore()
     for d in range(1, 4):
         pl.semaphore_signal(barrier, inc=1, device_id=x_peer(d), device_id_type=MESH)
-    for d in range(1, 8):
-        pl.semaphore_signal(barrier, inc=1, device_id=a_peer(d), device_id_type=MESH)
-        pl.semaphore_signal(barrier, inc=1, device_id=b_peer(d), device_id_type=MESH)
+    for d in range(1, 64):
+        pl.semaphore_signal(barrier, inc=1, device_id=c_peer(d), device_id_type=MESH)
 
     group = (lax.broadcasted_iota(jnp.int32, (8, 128), 1) // 8) % 4
     sub = lax.broadcasted_iota(jnp.int32, (8, 128), 0)
@@ -175,7 +180,7 @@
         cp.wait()
     build_weights(q_ref, w1_ref, 1)
 
-    pl.semaphore_wait(barrier, 17)
+    pl.semaphore_wait(barrier, 66)
     own_iq.wait()
     own_iw.wait()
 
@@ -247,26 +252,29 @@
         l_ref[...] = jnp.exp(top_ref[rows, :] - lse) * (1.0 / H)
         coef = [jnp.broadcast_to(l_ref[i : i + 1, :], (8, 128)) for i in range(8)]
 
-        @pl.loop(0, 8)
-        def _(b):
-            for k in range(32):
-                at = b * 32 + k
-                s = e_ref[c, at, 0] * coef[0]
-                for i in range(1, 8):
-                    s = s + e_ref[c, at, i] * coef[i]
-                u_ref[at] = s
-
-        for n in range(16):
-            v = u_ref[n * 16 : n * 16 + 16].reshape(128, 128).T
-            for k in range(4):
-                r = [v[32 * k + 8 * g : 32 * k + 8 * g + 8, :] for g in range(4)]
-                part_ref[c, k, :, n * 128 : (n + 1) * 128] = (r[0] + r[1]) + (r[2] + r[3])
-        for d in range(1, 4):
-            to = lax.rem(x + d, 4)
-            pltpu.make_async_remote_copy(
-                part_ref.at[c, to], got_ref.at[c, x],
-                r_send.at[c], r_recv.at[c], device_id=x_peer(d), device_id_type=MESH,
-            ).start()
+        for h in range(2):
+
+            @pl.loop(h * 4, h * 4 + 4)
+            def _(b):
+                for k in range(32):
+                    at = b * 32 + k
+                    s = e_ref[c, at, 0] * coef[0]
+                    for i in range(1, 8):
+                        s = s + e_ref[c, at, i] * coef[i]
+                    u_ref[at] = s
+
+            for n in range(8):
+                m = h * 8 + n
+                v = u_ref[m * 16 : m * 16 + 16].reshape(128, 128).T
+                for k in range(4):
+                    r = [v[32 * k + 8 * g : 32 * k + 8 * g + 8, :] for g in range(4)]
+                    part_ref[c, h, k, :, n * 128 : (n + 1) * 128] = (r[0] + r[1]) + (r[2] + r[3])
+            for d in range(1, 4):
+                to = lax.rem(x + d, 4)
+                pltpu.make_async_remote_copy(
+                    part_ref.at[c, h, to], got_ref.at[c, x, h],
+                    r_send.at[c], r_recv.at[c], device_id=x_peer(d), device_id_type=MESH,
+                ).start()
 
     def three(c):
         return pltpu.make_async_remote_copy(
@@ -276,14 +284,16 @@
 
     def own_rows(c):
         three(c).wait_recv()
-        got_ref[c, x] = part_ref[c, x]
+        for h in range(2):
+            got_ref[c, x, h] = part_ref[c, h, x]
         rows = slice(8 * c, 8 * c + 8)
         cross = [None] * 4
         mass = [None] * 4
         for n in range(16):
             at = slice(n * 128, (n + 1) * 128)
-            t = (got_ref[c, 0, :, at] + got_ref[c, 1, :, at]) + (
-                got_ref[c, 2, :, at] + got_ref[c, 3, :, at]
+            h, to = n // 8, slice(n % 8 * 128, n % 8 * 128 + 128)
+            t = (got_ref[c, 0, h, :, to] + got_ref[c, 1, h, :, to]) + (
+                got_ref[c, 2, h, :, to] + got_ref[c, 3, h, :, to]
             )
             tgt_ref[rows, at] = t
             positive = t > 0
@@ -398,10 +408,20 @@
         own_rows(c)
     spread = merge_lse(b_done(4))
     value = as_row(cm_ref[0]) + spread * as_row(cm_ref[1])
-    a_start(5, value)
-    b_start(5, jnp.sum(a_done(5), axis=0))
-    div_ref[...] = jnp.sum(b_done(5), axis=0)
-
+    fin_ref[me_c] = value[0:1]
+    for d in sorted(range(1, 64), key=lambda d: abs(d - 32)):
+        pltpu.make_async_remote_copy(
+            fin_ref.at[me_c], fin_ref.at[me_c], f_send.at[0], f_recv.at[0],
+            device_id=c_peer(d), device_id_type=MESH,
+        ).start()
+    others = pltpu.make_async_remote_copy(
+        fin_ref.at[pl.ds(0, 63)], fin_ref.at[pl.ds(0, 63)], f_send.at[0], f_recv.at[0],
+        device_id=x_peer(1), device_id_type=MESH,
+    )
+    others.wait_recv()
+    div_ref[...] = jnp.broadcast_to(jnp.sum(fin_ref[...], axis=0), (8, 128))
+
+    others.wait_send()
     for cp in ix_all():
         cp.wait_send()
     for e in range(NE):
@@ -447,8 +467,8 @@
             pltpu.VMEM((4, 4, 8, 16, 128), f32),
             pltpu.VMEM((32, KL), f32),
             pltpu.VMEM((KL // 8, 8, 128), f32),
-            pltpu.VMEM((4, 4, 8, KL), f32),
-            pltpu.VMEM((4, 4, 8, KL), f32),
+            pltpu.VMEM((4, 2, 4, 8, KL // 2), f32),
+            pltpu.VMEM((4, 4, 2, 8, KL // 2), f32),
             pltpu.VMEM((NE, 8, 8, 128), f32),
             pltpu.VMEM((NE, 8, 8, 128), f32),
             pltpu.VMEM((8, 128), f32),
@@ -456,8 +476,9 @@
             pltpu.VMEM((2, 32, 128), f32),
             pltpu.VMEM((128, KL), bf16),
             pltpu.VMEM((2, 4, 2, 64, 128), f32),
+            pltpu.VMEM((64, 1, 128), f32),
             dma((9,)), dma((2,)), dma((2,)), dma((2,)),
-            dma((NE,)), dma((NE,)), dma((NE,)), dma((NE,)), dma((4,)), dma((4,)),
+            dma((NE,)), dma((NE,)), dma((NE,)), dma((NE,)), dma((4,)), dma((4,)), dma((1,)), dma((1,)),
         ],
         compiler_params=pltpu.CompilerParams(
             collective_id=0, has_side_effects=True, vmem_limit_bytes=58_000_000

time: 55.2 us -> 53.7 us (0.973)
  Pallas kernels: 54.4 us -> 53 us
    pallas_call x1, Pallas kernels: 52.7 us -> 51.3 us  [local(): pl.pallas_call(kernel, out_shape=(jax.ShapeDtypeStruct((32, KL), f32), ja...]
where the time goes in v4:
time: 53.7 us; the launch traced here: 53.6 us
  Pallas kernels  53 us (99%)
  between operations  0.64 us (1%)
    pallas_call x1, Pallas kernels, local(): pl.pallas_call(kernel, out_shape=(jax.ShapeDtypeStruct((32, KL), f32), ja...  51.3 us
    pallas_call x1, Pallas kernels, local(): pl.pallas_call(results, out_shape=(jax.ShapeDtypeStruct((32, KL), f32), j...  1.68 us

profile of v4, /device:TPU:1, one launch (start us, length us, event | category | flops | bytes accessed | tf_op | source)
XLA Modules:
  0.0 53.6 jit_solution(2886075778319790597)
XLA Ops:
  0.6 51.3 %shard_map.77 = (f32[32,2048]{1,0:T(8,128)}, f32[8,128]{1,0:T(8,128)}) custom-call(s32[128]{0:T(128)} %pos_s.1, s32[1,128]{1,0:T(1,128)} %bitcast.9, bf16[32,576,128]{2,1,0:T(8,128)(2,1)} %bitcast.5, bf16[576,2048]{1,0:T(8,128)(2,1)} %bitcast.6, bf16[16,8,16,128]{3,2,1,0:T(8,128)(2,1)} %bitcast.7, bf16[16,128]{1,0:T(8,128)(2,1)} %bitcast.8, ...), custom_call_target="tpu_custom_call" | custom-call | tf_op jit(solution)/shard_map/pallas_call | solution.py:444
  51.9 1.7 %shard_map.78 = (f32[32,2048]{1,0:T(8,128)}, f32[32]{0:T(128)}) custom-call(f32[32,2048]{1,0:T(8,128)} %get-tuple-element.4.sum_ref, f32[8,128]{1,0:T(8,128)} %get-tuple-element.5.row_ref), custom_call_target="tpu_custom_call" | custom-call | tf_op jit(solution)/shard_map/pallas_call | solution.py:495

commit v5 on v4

--- a/solution.py
+++ b/solution.py
@@ -351,7 +351,7 @@
             wc_ref[q // 8, k, q % 8] = jnp.broadcast_to(w[:, q : q + 1], (16, 128))
 
     def logits_block(n, s):
-        at = pl.ds(pl.multiple_of(n * 256, 256), 256)
+        at = pl.ds(n * 256 if isinstance(n, int) else pl.multiple_of(n * 256, 256), 256)
         keys = ikt_ref[:, at]
         for b in range(4):
             r = lax.dot_general(
@@ -374,16 +374,17 @@
                 v = f_ref[s, b, j, pl.ds(0, 8, stride=8), :]
                 for i in range(1, 8):
                     v = v + f_ref[s, b, j, pl.ds(i, 8, stride=8), :]
-                lg_ref[8 * b : 8 * b + 8, pl.ds(pl.multiple_of(n * 256 + j * 128, 128), 128)] = v
-
-    @pl.loop(0, 2)
-    def _(n):
-        logits_block(n * 2, 0)
-        logits_block(n * 2 + 1, 1)
+                lg_ref[8 * b : 8 * b + 8, pl.ds(
+                    n * 256 + j * 128 if isinstance(n, int)
+                    else pl.multiple_of(n * 256 + j * 128, 128), 128,
+                )] = v
+
+    logits_block(0, 0)
+    logits_block(1, 1)
 
     middle(3)
 
-    @pl.loop(2, 4)
+    @pl.loop(1, 4)
     def _(n):
         logits_block(n * 2, 0)
         logits_block(n * 2 + 1, 1)
@@ -418,10 +419,6 @@
         fin_ref.at[pl.ds(0, 63)], fin_ref.at[pl.ds(0, 63)], f_send.at[0], f_recv.at[0],
         device_id=x_peer(1), device_id_type=MESH,
     )
-    others.wait_recv()
-    div_ref[...] = jnp.broadcast_to(jnp.sum(fin_ref[...], axis=0), (8, 128))
-
-    others.wait_send()
     for cp in ix_all():
         cp.wait_send()
     for e in range(NE):
@@ -429,6 +426,9 @@
         seven(bb_ref, e, b_send, b_recv).wait_send()
     for c in range(4):
         three(c).wait_send()
+    others.wait_recv()
+    div_ref[...] = jnp.broadcast_to(jnp.sum(fin_ref[...], axis=0), (8, 128))
+    others.wait_send()
 
 
 def results(sum_ref, row_ref, tgt_ref, div_ref):

time: 53.7 us -> 53.4 us (level)
  no operation moved by 1% of the time
where the time goes in v5:
time: 53.4 us; the launch traced here: 53.3 us
  Pallas kernels  52.6 us (99%)
  between operations  0.64 us (1%)
    pallas_call x1, Pallas kernels, local(): pl.pallas_call(kernel, out_shape=(jax.ShapeDtypeStruct((32, KL), f32), ja...  50.9 us
    pallas_call x1, Pallas kernels, local(): pl.pallas_call(results, out_shape=(jax.ShapeDtypeStruct((32, KL), f32), j...  1.68 us

profile of v5, /device:TPU:1, one launch (start us, length us, event | category | flops | bytes accessed | tf_op | source)
XLA Modules:
  0.0 53.3 jit_solution(14872527216644527500)
XLA Ops:
  0.6 50.9 %shard_map.77 = (f32[32,2048]{1,0:T(8,128)}, f32[8,128]{1,0:T(8,128)}) custom-call(s32[128]{0:T(128)} %pos_s.1, s32[1,128]{1,0:T(1,128)} %bitcast.9, bf16[32,576,128]{2,1,0:T(8,128)(2,1)} %bitcast.5, bf16[576,2048]{1,0:T(8,128)(2,1)} %bitcast.6, bf16[16,8,16,128]{3,2,1,0:T(8,128)(2,1)} %bitcast.7, bf16[16,128]{1,0:T(8,128)(2,1)} %bitcast.8, ...), custom_call_target="tpu_custom_call" | custom-call | tf_op jit(solution)/shard_map/pallas_call | solution.py:444
  51.6 1.7 %shard_map.78 = (f32[32,2048]{1,0:T(8,128)}, f32[32]{0:T(128)}) custom-call(f32[32,2048]{1,0:T(8,128)} %get-tuple-element.4.sum_ref, f32[8,128]{1,0:T(8,128)} %get-tuple-element.5.row_ref), custom_call_target="tpu_custom_call" | custom-call | tf_op jit(solution)/shard_map/pallas_call | solution.py:495
